TPU v7x, 32 devices: a whole 2x2x4 slice. The times are simulated.
32 devices in a mesh: seq: 16 (over z, y, x), batch: 2 (over core).
Axes of the slice: x: 2, y: 2, z: 4, core: 2. Of those that a mesh axis runs over, the one named last changes fastest.
Arguments:
- inputs: bfloat16 [2, 2048, 2048], P('batch', 'seq'), may hold values from -6 to 6
- cotangent: bfloat16 [2, 2048, 1024], P('batch', 'seq'), may hold values from -48 to 48
- w_query: bfloat16 [2048, 128], replicated, may hold values from -0.125 to 0.125
- w_key: bfloat16 [2048, 128], replicated, may hold values from -0.125 to 0.125
- w_value: bfloat16 [2048, 1024], replicated, may hold values from -0.125 to 0.125
Outputs:
- grad_inputs: bfloat16 [2, 2048, 2048], P('batch', 'seq')
- grad_w_query: float32 [2048, 128], P(('seq', 'batch'))
- grad_w_key: float32 [2048, 128], P(('seq', 'batch'))
- grad_w_value: float32 [2048, 1024], P(('seq', 'batch'))
All inputs are finite; a program needn't handle non-finite values.
Results may differ from a plain program's by a relative error of at most 0.006.
Values sent between devices are 32-bit elements; how exact they have to be, the bound alone decides.
A program may use at most 128 MiB of HBM per device.

v0:
```python
import math

import jax
import jax.numpy as jnp
import numpy as np
from jax import lax
from jax.sharding import PartitionSpec as P

H = 8
DK = 16
DV = 128


highest = lax.Precision.HIGHEST
threepass = lax.Precision.HIGH


def prefix(part, axis, combine, identity, reverse):
    count = lax.axis_size(axis)
    place = lax.axis_index(axis)
    ahead = count - 1 - place if reverse else place
    gathered = jax.tree.map(lambda a: lax.all_gather(a, axis), part)
    state = jax.tree.map(lambda a, e: jnp.zeros_like(a) + jnp.asarray(e, a.dtype), part, identity)

    def one(step, state):
        source = count - 1 - step if reverse else step
        return combine(
            state, jax.tree.map(lambda a: lax.dynamic_index_in_dim(a, source, 0, False), gathered)
        )

    return lax.fori_loop(0, ahead, one, state)


def pair_tables(width):
    rows_idx, cols_idx = np.triu_indices(width)
    eye_table = np.eye(width, dtype=np.float32)
    left_pick = jnp.asarray(eye_table[rows_idx])
    right_pick = jnp.asarray(eye_table[cols_idx])
    pair_coef = jnp.asarray(
        np.where(rows_idx == cols_idx, 1.0 / math.sqrt(2.0), 1.0).astype(np.float32)
    )
    return (left_pick, right_pick, pair_coef)


def features(scaled, tables):
    left_pick, right_pick, pair_coef = tables
    left_val = jnp.einsum("...d,pd->...p", scaled, left_pick, precision=highest)
    right_val = jnp.einsum("...d,pd->...p", scaled, right_pick, precision=highest)
    leading = jnp.ones(scaled.shape[:-1] + (1,), jnp.float32)
    return jnp.concatenate([leading, scaled, left_val * right_val * pair_coef], -1)


def pull_back(scaled, grad_feat, tables):
    left_pick, right_pick, pair_coef = tables
    width = scaled.shape[-1]
    linear_part = grad_feat[..., 1 : 1 + width]
    pair_grad = grad_feat[..., 1 + width :] * pair_coef
    left_val = jnp.einsum("...d,pd->...p", scaled, left_pick, precision=highest)
    right_val = jnp.einsum("...d,pd->...p", scaled, right_pick, precision=highest)
    result = linear_part + jnp.einsum(
        "...p,pd->...d", pair_grad * right_val, left_pick, precision=highest
    )
    return result + jnp.einsum("...p,pd->...d", pair_grad * left_val, right_pick, precision=highest)


def add_pair(earlier, later):
    return (earlier[0] + later[0], earlier[1] + later[1])


def times_transposed(left, right):
    return lax.dot_general(
        left, right, (((1,), (1,)), ((), ())), preferred_element_type=jnp.float32
    )


def body(inputs, cotangent, w_query, w_key, w_value):
    tables = pair_tables(DK)
    tokens = inputs[0]
    length = tokens.shape[0]
    query = jnp.dot(tokens, w_query, preferred_element_type=jnp.float32).reshape(length, H, DK)
    keys = jnp.dot(tokens, w_key, preferred_element_type=jnp.float32).reshape(length, H, DK)
    values = (
        jnp.dot(tokens, w_value, preferred_element_type=jnp.float32)
        .astype(jnp.bfloat16)
        .reshape(length, H, DV)
    )
    feat_q = features(query * 0.5, tables).astype(jnp.bfloat16)
    feat_k = features(keys * 0.5, tables).astype(jnp.bfloat16)
    upstream = cotangent[0].astype(jnp.float32).reshape(length, H, DV)
    fq32 = feat_q.astype(jnp.float32)
    fk32 = feat_k.astype(jnp.float32)
    val32 = values.astype(jnp.float32)
    causal = lax.broadcasted_iota(jnp.int32, (length, length), 0) >= lax.broadcasted_iota(
        jnp.int32, (length, length), 1
    )
    attn = jnp.einsum("thf,shf->hts", feat_q, feat_k, preferred_element_type=jnp.float32)
    attn = jnp.where(causal, attn, 0.0)
    local_state = jnp.einsum("shf,she->hfe", feat_k, values, preferred_element_type=jnp.float32)
    local_norm = jnp.sum(fk32, 0)
    zero_pair = (jnp.zeros_like(local_state), jnp.zeros_like(local_norm))
    state, norm_state = prefix((local_state, local_norm), "seq", add_pair, zero_pair, False)
    numerator = jnp.einsum("hts,she->the", attn, val32, precision=threepass)
    numerator = numerator + jnp.einsum("thf,hfe->the", fq32, state, precision=threepass)
    denominator = jnp.transpose(jnp.sum(attn, -1), (1, 0))
    denominator = denominator + jnp.einsum("thf,hf->th", fq32, norm_state, precision=highest)
    output = numerator / denominator[..., None]
    grad_numer = upstream / denominator[..., None]
    grad_denom = -jnp.sum(upstream * output, -1) / denominator
    grad_attn = jnp.einsum("the,she->hts", grad_numer, val32, precision=threepass)
    grad_attn = jnp.where(causal, grad_attn + jnp.transpose(grad_denom, (1, 0))[:, :, None], 0.0)
    grad_fq = jnp.einsum("hts,shf->thf", grad_attn, fk32, precision=threepass)
    grad_fq = grad_fq + jnp.einsum("hfe,the->thf", state, grad_numer, precision=threepass)
    grad_fq = grad_fq + norm_state[None, :, :] * grad_denom[..., None]
    local_back = jnp.einsum("thf,the->hfe", fq32, grad_numer, precision=threepass)
    local_back_norm = jnp.einsum("thf,th->hf", fq32, grad_denom, precision=highest)
    back_state, back_norm = prefix((local_back, local_back_norm), "seq", add_pair, zero_pair, True)
    grad_val = jnp.einsum("hts,the->she", attn, grad_numer, precision=threepass)
    grad_val = grad_val + jnp.einsum("shf,hfe->she", fk32, back_state, precision=threepass)
    grad_fk = jnp.einsum("hts,thf->shf", grad_attn, fq32, precision=threepass)
    grad_fk = grad_fk + jnp.einsum("she,hfe->shf", val32, back_state, precision=threepass)
    grad_fk = grad_fk + back_norm[None, :, :]
    grad_query = (
        (pull_back(query * 0.5, grad_fq, tables) * 0.5).astype(jnp.bfloat16).reshape(length, H * DK)
    )
    grad_keys = (
        (pull_back(keys * 0.5, grad_fk, tables) * 0.5).astype(jnp.bfloat16).reshape(length, H * DK)
    )
    grad_values = grad_val.astype(jnp.bfloat16).reshape(length, H * DV)
    grad_in = (
        times_transposed(grad_query, w_query)
        + times_transposed(grad_keys, w_key)
        + times_transposed(grad_values, w_value)
    )
    grad_in = grad_in.astype(jnp.bfloat16)[None]
    joined_grads = jnp.concatenate([grad_query, grad_keys, grad_values], 1)
    reduced = lax.psum_scatter(
        lax.dot_general(
            tokens, joined_grads, (((0,), (0,)), ((), ())), preferred_element_type=jnp.float32
        ),
        ("seq", "batch"),
        scatter_dimension=0,
        tiled=True,
    )
    grad_wq = reduced[:, : H * DK]
    grad_wk = reduced[:, H * DK : 2 * H * DK]
    grad_wv = reduced[:, 2 * H * DK :]
    return (grad_in, grad_wq, grad_wk, grad_wv)


def solution(mesh):
    in_specs = (P("batch", "seq", None), P("batch", "seq", None), P(), P(), P())
    out_specs = (
        P("batch", "seq", None),
        P(("seq", "batch"), None),
        P(("seq", "batch"), None),
        P(("seq", "batch"), None),
    )
    return jax.shard_map(body, mesh=mesh, in_specs=in_specs, out_specs=out_specs, check_vma=False)
```

profile of v0, /device:TPU:0, one launch (start us, length us, event | category | flops | bytes accessed | tf_op | source)
XLA Modules:
  0.0 577.6 jit_solution(15588852291930751092)
XLA Ops:
  7.3 1.3 copy.48
  8.9 1.4 fusion.55
  10.2 1.4 fusion.56
  11.6 1.2 copy.50
  13.2 1.4 fusion.57
  14.5 2.9 fusion.14
  17.5 1.5 multiply_convert_fusion
  19.3 1.2 copy.52
  22.0 46.4 %all-gather.1 = f32[128,153]{1,0:T(8,128)} all-gather(f32[8,153]{1,0:T(8,128)S(1)} %convert_reduce_fusion), channel_id=3, replica_groups=mesh['seq'=16,'batch'=2] {'seq'}, dimensions={0}, use_global_device_ids=true | all-gather | bytes 83232 | tf_op jit(solution)/shard_map/all_gather | solution.py:22
  69.4 1.3 fusion.54
  70.6 107.7 %all-gather.7.cloned.1.call-done = f32[128,153,128]{2,0,1:T(8,128)} async-done(((f32[8,153,128]{2,0,1:T(8,128)}), f32[128,153,128]{2,0,1:T(8,128)}) %all-gather.7.cloned.1.call-update) | async-done | bytes 10027024 | tf_op jit(solution)/shard_map/all_gather | solution.py:22
  178.4 1.3 fusion.46
  179.8 1.7 fusion.50
  181.4 1.2 copy.63
  182.8 1.5 fusion.36
  184.3 2.0 fusion.13
  186.3 1.6 fusion.60
  187.9 72.4 %all-gather.3 = f32[128,153]{1,0:T(8,128)} all-gather(f32[8,153]{1,0:T(8,128)S(1)} %bitcast.160), channel_id=5, replica_groups=mesh['seq'=16,'batch'=2] {'seq'}, dimensions={0}, use_global_device_ids=true | all-gather | bytes 83232 | tf_op jit(solution)/shard_map/all_gather | solution.py:22
  260.3 1.4 fusion.11
  261.7 1.5 convolution_bitcast_fusion.1
  264.1 1.2 fusion.17
  265.8 1.5 fusion.49
  267.3 99.2 %all-gather.9.cloned.1.call-done = f32[128,153,128]{2,0,1:T(8,128)} async-done(((f32[8,153,128]{2,0,1:T(8,128)}), f32[128,153,128]{2,0,1:T(8,128)}) %all-gather.9.cloned.1.call-update) | async-done | bytes 10027024 | tf_op jit(solution)/shard_map/all_gather | solution.py:22
  366.6 30.7 %while.27 = (s32[]{:T(128)}, f32[8,153,128]{2,1,0:T(8,128)S(1)}, f32[8,153]{1,0:T(8,128)S(1)}, s32[]{:T(128)}, f32[16,8,153,128]{3,1,0,2:T(8,128)}, /*index=5*/f...) while((s32[]{:T(128)}, f32[8,153,128]{2,1,0:T(8,128)S(1)}, f32[8,153]{1,0:T(8,128)S(1)}, ...), condition=%wide.region_6.7_spmd, body=%wide.region_5.6_spmd.sunk | while | flops 157902 | bytes 3148283 | solution.py:31
  366.6 1.1 constant_dynamic-slice_fusion.5
  368.6 1.1 constant_dynamic-slice_fusion.5
  370.7 1.1 constant_dynamic-slice_fusion.5
  372.7 1.1 constant_dynamic-slice_fusion.5
  374.8 1.1 constant_dynamic-slice_fusion.5
  376.8 1.1 constant_dynamic-slice_fusion.5
  378.9 1.1 constant_dynamic-slice_fusion.5
  380.9 1.1 constant_dynamic-slice_fusion.5
  383.0 1.1 constant_dynamic-slice_fusion.5
  385.0 1.1 constant_dynamic-slice_fusion.5
  387.1 1.1 constant_dynamic-slice_fusion.5
  389.1 1.1 constant_dynamic-slice_fusion.5
  391.1 1.1 constant_dynamic-slice_fusion.5
  393.2 1.1 constant_dynamic-slice_fusion.5
  395.2 1.1 constant_dynamic-slice_fusion.5
  397.3 1.9 fusion.12
  400.2 1.3 fusion.18
  401.5 6.1 %convolution_bitcast_fusion = f32[2048,1280]{0,1:T(8,128)} fusion(bf16[1,128,2048]{2,1,0:T(8,128)(2,1)S(1)} %copy-done, bf16[128,1024]{0,1:T(8,128)(2,1)S(1)} %bitcast.138, bf16[128,128]{0,1:T(8,128)(2,1)S(1)} %bitcast.150, bf16[128,128]{0,1:T(8,128)(2,1)} %bitcast.148), kind=kOutput, calls=%fused_computation.8 | convolution fusion | flops 672071680 | bytes 11337728 | tf_op jit(solution)/shard_map/dot_general | solution.py:137
  407.6 11.3 %copy.82 = f32[2048,1280]{1,0:T(8,128)} copy(f32[2048,1280]{0,1:T(8,128)} %convolution_bitcast_fusion) | data formatting | bytes 20971520
  418.9 1.0 copy-done.6
  420.6 4.6 fusion.3
  425.2 142.8 %reduce-scatter.4.cloned.1.call-done = f32[64,1280]{1,0:T(8,128)} async-done(((f32[2048,1280]{1,0:T(8,128)}), f32[64,1280]{1,0:T(8,128)}) %reduce-scatter.4.cloned.1.call-update) | async-done | bytes 327696
  568.0 1.7 slice.34
  569.6 1.4 fusion.51
  (89 shorter events, 20.4 us)
Async XLA Ops:
  7.2 1.4 copy-start
  7.2 10.3 %copy-start.11 = (f32[136,16,1]{0,1,2:T(8,128)S(1)}, f32[136,16,1]{0,1,2:T(8,128)}, u32[]{:S(2)}) copy-start(f32[136,16,1]{0,1,2:T(8,128)} %constant.70) | copy-start | bytes 26116
  7.2 10.3 %copy-start.14 = (f32[136]{0:T(256)S(1)}, f32[136]{0:T(256)}, u32[]{:S(2)}) copy-start(f32[136]{0:T(256)} %constant.67.clone) | copy-start | bytes 1636
  7.2 13.4 %copy-start.13 = (bf16[1,128,1024]{2,1,0:T(8,128)(2,1)S(1)}, bf16[1,128,1024]{2,1,0:T(8,128)(2,1)}, u32[]{:S(2)}) copy-start(bf16[1,128,1024]{2,1,0:T(8,128)(2,1)} %param.13) | copy-start | bytes 786436
  7.2 171.1 %all-gather.7.cloned.1.call-start = ((), (), s32[]{:S(2)}) async-start(), calls=%async_computation.1 | async-start | bytes 10653696 | tf_op jit(solution)/shard_map/all_gather | solution.py:22
  20.6 345.9 %all-gather.9.cloned.1.call-start = ((), (), s32[]{:S(2)}) async-start(), calls=%async_computation.2 | async-start | bytes 10653696 | tf_op jit(solution)/shard_map/all_gather | solution.py:22
  68.6 0.7 copy-start.1
  178.4 85.7 %copy-start.12 = (f32[136,16,1]{0,1,2:T(8,128)S(1)}, f32[136,16,1]{0,1,2:T(8,128)}, u32[]{:S(2)}) copy-start(f32[136,16,1]{0,1,2:T(8,128)} %constant.71) | copy-start | bytes 26116
  182.7 385.3 %reduce-scatter.4.cloned.1.call-start = ((), (), s32[]{:S(2)}) async-start(), calls=%async_computation.3 | async-start | bytes 10813440
  182.7 81.4 %copy-start.5 = (f32[128,8,136]{0,2,1:T(8,128)S(1)}, f32[128,8,136]{0,2,1:T(8,128)}, u32[]{:S(2)}) copy-start(f32[128,8,136]{0,2,1:T(8,128)} %get-tuple-element.175) | copy-start | bytes 1671172
  182.7 82.5 %copy-start.2 = (bf16[128,8,153]{0,2,1:T(8,128)(2,1)S(1)}, bf16[128,8,153]{0,2,1:T(8,128)(2,1)}, u32[]{:S(2)}) copy-start(bf16[128,8,153]{0,2,1:T(8,128)(2,1)} %copy-done.1) | copy-start | bytes 940036
  182.8 83.0 %copy-start.8 = (f32[1,128,1024]{1,2,0:T(8,128)S(1)}, f32[1,128,1024]{1,2,0:T(8,128)}, u32[]{:S(2)}) copy-start(f32[1,128,1024]{1,2,0:T(8,128)} %copy.49) | copy-start | bytes 1572868
  182.8 83.0 %copy-start.9 = (f32[8,128,128]{1,2,0:T(8,128)S(1)}, f32[8,128,128]{1,2,0:T(8,128)}, u32[]{:S(2)}) copy-start(f32[8,128,128]{1,2,0:T(8,128)} %get-tuple-element.181) | copy-start | bytes 1572868
  399.2 2.3 copy-start.3
  418.9 1.0 copy-start.6
  418.9 1.0 copy-start.10
  418.9 1.4 copy-start.7
  418.9 1.7 copy-start.4
Sparse Core Ops, SparseCore 0:
  20.7 157.6 all-gather.6
  182.8 183.6 all-gather.8
  419.1 148.8 reduce-scatter.3
where the time goes:
time: 580 us; the launch traced here: 578 us
  waiting for transfers between devices  350 us (60%)
  blocking collectives  119 us (21%)
  matrix products  41 us (7%)
  local copies, waits for them, and re-layouts  39 us (7%)
  other arithmetic  14.4 us (2%)
  between operations  14.1 us (2%)
    all_gather x2, waiting for transfers between devices, prefix(): gathered = jax.tree.map(lambda a: lax.all_gather(a, axis), part)  207 us
    unnamed x4, waiting for transfers between devices  143 us
    all_gather x2, blocking collectives, prefix(): gathered = jax.tree.map(lambda a: lax.all_gather(a, axis), part)  119 us
    dynamic_slice x15, local copies, waits for them, and re-layouts, one(): lax.dynamic_index_in_dim(a, source, 0, False)  16.8 us
    unnamed x33, local copies, waits for them, and re-layouts  15.7 us
    add x30, other arithmetic, add_pair(): return (earlier[0] + later[0], earlier[1] + later[1])  13.8 us
  transfers between devices with their start and end apart: 3, of which 3 were waited for; matrix products, arithmetic and copies ran while one was open for 3% of the time, Pallas kernels for 0%

commit v1 on v0

v1 whole, which is shorter than its diff:
```python
import functools
import math

import jax
import jax.numpy as jnp
import numpy as np
from jax import lax
from jax.experimental import pallas as pl
from jax.experimental.pallas import tpu as pltpu
from jax.sharding import PartitionSpec as P

H = 8
DK = 16
DV = 128
AUX = 16
MESH = pl.DeviceIdType.MESH
BF = jnp.bfloat16
F32 = jnp.float32


def group(kind, outer, inner):
    seq = lax.axis_index("seq")
    core = lax.axis_index("batch")
    high = seq // inner
    low = seq % inner
    if kind == "seq":
        return outer * inner, seq, lambda j: (j, core)
    if kind == "plane":
        return inner * 2, low * 2 + core, lambda j: (high * inner + j // 2, j % 2)
    if kind == "line":
        return outer, high, lambda j: (j * inner + low, core)
    return 2, core, lambda j: (seq, j)


def exchange_kernel(kinds, outer, inner, *refs):
    count = len(kinds)
    ins, outs = refs[:count], refs[count : 2 * count]
    sends, recvs = refs[2 * count : 3 * count], refs[3 * count :]
    groups = [group(kind, outer, inner) for kind in kinds]
    barrier = pltpu.get_barrier_semaphore()
    total = 0
    for size, me, where in groups:
        for k in range(1, size):
            pl.semaphore_signal(
                barrier, inc=1, device_id=where((me + k) % size), device_id_type=MESH
            )
        total += size - 1
    pl.semaphore_wait(barrier, total)
    copies = []
    for (size, me, where), src, dst, send, recv in zip(groups, ins, outs, sends, recvs):
        for k in range(1, size):
            peer = (me + k) % size
            copy = pltpu.make_async_remote_copy(
                src_ref=src.at[peer],
                dst_ref=dst.at[me],
                send_sem=send.at[k],
                recv_sem=recv.at[k],
                device_id=where(peer),
                device_id_type=MESH,
            )
            copy.start()
            copies.append(copy)
    for (size, me, where), src, dst in zip(groups, ins, outs):
        dst[me] = src[me]
    for copy in copies:
        copy.wait()


def exchange(arrays, kinds, outer, inner, number):
    sizes = {"seq": outer * inner, "plane": inner * 2, "line": outer, "pair": 2}
    sems = [pltpu.SemaphoreType.DMA((sizes[k],)) for k in kinds]
    return pl.pallas_call(
        functools.partial(exchange_kernel, kinds, outer, inner),
        out_shape=[jax.ShapeDtypeStruct(a.shape, a.dtype) for a in arrays],
        in_specs=[pl.BlockSpec(memory_space=pltpu.VMEM)] * len(arrays),
        out_specs=[pl.BlockSpec(memory_space=pltpu.VMEM)] * len(arrays),
        scratch_shapes=sems + sems,
        compiler_params=pltpu.CompilerParams(
            collective_id=number, has_side_effects=True, vmem_limit_bytes=60 << 20
        ),
    )(*arrays)


def dot(left, right, dims):
    return lax.dot_general(left, right, ((dims[:1], dims[1:]), ((), ())), preferred_element_type=F32)


def halves(a):
    high = a.astype(BF)
    return high, (a - high.astype(F32)).astype(BF)


def dot2(pair, right, dims):
    return dot(pair[0], right, dims) + dot(pair[1], right, dims)


def dot2r(left, pair, dims):
    return dot(left, pair[0], dims) + dot(left, pair[1], dims)


def dot3(lefts, rights, dims):
    return (
        dot(lefts[0], rights[0], dims)
        + dot(lefts[0], rights[1], dims)
        + dot(lefts[1], rights[0], dims)
    )


def coefs():
    table = np.where(np.eye(DK) > 0, 1.0 / math.sqrt(2.0), 1.0).astype(np.float32)
    table = table * (np.arange(DK)[:, None] <= np.arange(DK)[None, :])
    half = DK // 2
    rows = np.concatenate([table[:half].reshape(-1), table[half:, half:].reshape(-1)])
    return np.ascontiguousarray(np.broadcast_to(rows[:, None], (rows.size, 128)))


def phi(u, coef):
    half = DK // 2
    lanes = u.shape[1]
    pieces = []
    for i in range(DK):
        low = u if i < half else u[half:]
        pieces.append(u[i : i + 1] * low)
    pairs = jnp.concatenate(pieces, 0) * coef
    first = (lax.broadcasted_iota(jnp.int32, (AUX, lanes), 0) == 0).astype(F32)
    return jnp.concatenate([pairs, u, first], 0)


def pull(u, grad, coef):
    half = DK // 2
    pairs = grad[: coef.shape[0]] * coef
    linear = grad[coef.shape[0] : coef.shape[0] + DK]
    rows = lax.broadcasted_iota(jnp.int32, u.shape, 0)
    total = linear
    lower = jnp.zeros_like(u[half:])
    at = 0
    for i in range(DK):
        if i < half:
            piece = pairs[at : at + DK]
            at += DK
            total = total + piece * u[i : i + 1]
            mine = jnp.sum(piece * u, 0, keepdims=True)
        else:
            piece = pairs[at : at + half]
            at += half
            lower = lower + piece * u[i : i + 1]
            mine = jnp.sum(piece * u[half:], 0, keepdims=True)
        total = total + jnp.where(rows == i, mine, 0.0)
    return total + jnp.concatenate([jnp.zeros_like(lower), lower], 0)


def attention_kernel(wide, r_ref, c_ref, o_ref, fq_ref, fk_ref, va_ref, ah, al, gh, gl, nh, nl):
    blocks, _, tokens = r_ref.shape
    length = 2 * tokens
    chunks = blocks // 2
    feats = fq_ref.shape[1]
    coef = jnp.concatenate([c_ref[...]] * (length // 128), 1)
    causal = lax.broadcasted_iota(jnp.int32, (length, length), 0) <= lax.broadcasted_iota(
        jnp.int32, (length, length), 1
    )
    aux_row = lax.broadcasted_iota(jnp.int32, (AUX, length), 0) == 0

    def block(c):
        return jnp.concatenate([r_ref[2 * c], r_ref[2 * c + 1]], 1)

    def store(c, start, rows):
        size = rows.shape[0]
        o_ref[2 * c, start : start + size, :] = rows[:, :tokens]
        o_ref[2 * c + 1, start : start + size, :] = rows[:, tokens:]

    def forward(c, state):
        both = block(c)
        uq = both[:DK] * 0.5
        uk = both[DK : 2 * DK] * 0.5
        val = both[2 * DK : 2 * DK + wide]
        up = both[2 * DK + wide :]
        fq = phi(uq, coef).astype(BF)
        fk = phi(uk, coef).astype(BF)
        va = jnp.concatenate([val, aux_row.astype(F32)], 0).astype(BF)
        fq_ref[c] = fq
        fk_ref[c] = fk
        va_ref[c] = va
        attn = halves(jnp.where(causal, dot(fk, fq, (0, 0)), 0.0))
        ah[c] = attn[0]
        al[c] = attn[1]
        held = halves(state)
        top = dot2r(va, attn, (1, 0)) + dot2(held, fq, (1, 0))
        scale = 1.0 / top[wide : wide + 1]
        numer = up * scale
        denom = -jnp.sum(numer * top[:wide], 0, keepdims=True) * scale
        gn = halves(jnp.concatenate([numer, jnp.where(aux_row, denom, 0.0)], 0))
        nh[c] = gn[0]
        nl[c] = gn[1]
        ga = halves(jnp.where(causal, dot2r(va, gn, (0, 0)), 0.0))
        gh[c] = ga[0]
        gl[c] = ga[1]
        gfq = dot2r(fk, ga, (1, 0)) + dot3(held, gn, (0, 0))
        store(c, 0, pull(uq, gfq, coef) * 0.5)
        return state + dot(va, fk, (1, 1))

    zero = jnp.zeros((wide + AUX, feats), F32)
    lax.fori_loop(0, chunks, forward, zero)

    def backward(step, state):
        c = chunks - 1 - step
        uk = block(c)[DK : 2 * DK] * 0.5
        fq, fk, va = fq_ref[c], fk_ref[c], va_ref[c]
        attn = (ah[c], al[c])
        ga = (gh[c], gl[c])
        gn = (nh[c], nl[c])
        held = halves(state)
        gv = dot3(gn, attn, (1, 1)) + dot2(held, fk, (1, 0))
        store(c, 2 * DK, gv[:wide])
        gfk = dot2r(fq, ga, (1, 1)) + dot2(held, va, (0, 0))
        store(c, DK, pull(uk, gfk, coef) * 0.5)
        return state + dot2(gn, fq, (1, 1))

    lax.fori_loop(0, chunks, backward, zero)


def attention(received, wide):
    blocks, _, tokens = received.shape
    coef = coefs()
    feats = coef.shape[0] + DK + AUX
    chunks, length = blocks // 2, 2 * tokens
    square = pltpu.VMEM((chunks, length, length), BF)
    grads = pltpu.VMEM((chunks, wide + AUX, length), BF)
    feat = pltpu.VMEM((chunks, feats, length), BF)
    return pl.pallas_call(
        functools.partial(attention_kernel, wide),
        out_shape=jax.ShapeDtypeStruct((blocks, 2 * DK + wide, tokens), F32),
        in_specs=[pl.BlockSpec(memory_space=pltpu.VMEM)] * 2,
        out_specs=pl.BlockSpec(memory_space=pltpu.VMEM),
        scratch_shapes=[feat, feat, grads, square, square, square, square, grads, grads],
        compiler_params=pltpu.CompilerParams(vmem_limit_bytes=60 << 20),
    )(received, jnp.asarray(coef))


def body(inputs, cotangent, w_query, w_key, w_value):
    seqs = lax.axis_size("seq")
    outer = 4 if seqs % 4 == 0 else 1
    inner = seqs // outer
    split = seqs // H
    wide = DV // split
    tokens = inputs[0]
    length, width = tokens.shape
    weights = jnp.concatenate([w_query, w_key, w_value], 1)
    cols = weights.shape[1]
    qk = H * DK
    proj = lax.dot_general(weights, tokens, (((0,), (1,)), ((), ())), preferred_element_type=F32)
    heads = proj[: 2 * qk].reshape(2, H, 1, DK, length)
    heads = jnp.broadcast_to(heads, (2, H, split, DK, length)).reshape(2, seqs, DK, length)
    values = proj[2 * qk :].astype(BF).astype(F32).reshape(seqs, wide, length)
    upstream = cotangent[0].astype(F32).T.reshape(seqs, wide, length)
    sent = jnp.concatenate([heads[0], heads[1], values, upstream], 1)
    rows = width // seqs
    staged = tokens.astype(F32).reshape(length, outer, inner, rows).transpose(2, 0, 1, 3)
    staged = staged.reshape(inner, 1, length, outer * rows)
    staged = jnp.broadcast_to(staged, (inner, 2, length, outer * rows))
    staged = staged.reshape(inner * 2, length, outer * rows)
    received, group_in = exchange([sent, staged], ["seq", "plane"], outer, inner, 0)
    back = attention(received, wide)
    (grads,) = exchange([back], ["seq"], outer, inner, 1)
    small = grads[:, : 2 * DK].reshape(H, split, 2, DK, length).sum(1)
    small = small.transpose(1, 0, 2, 3).reshape(2 * qk, length)
    joined = jnp.concatenate([small, grads[:, 2 * DK :].reshape(H * DV, length)], 0).astype(BF)
    grad_in = lax.dot_general(
        joined, weights, (((0,), (1,)), ((), ())), preferred_element_type=F32
    ).astype(BF)[None]
    part = joined.astype(F32).reshape(1, 2, cols // 2, length)
    part = jnp.broadcast_to(part, (inner, 2, cols // 2, length)).reshape(
        inner * 2, cols // 2, length
    )
    (group_grad,) = exchange([part], ["plane"], outer, inner, 2)
    partial = jnp.einsum(
        "gtr,gct->rc", group_in.astype(BF), group_grad.astype(BF), preferred_element_type=F32
    )
    (lined,) = exchange([partial.reshape(outer, rows, cols // 2)], ["line"], outer, inner, 3)
    summed = lined.sum(0).reshape(2, rows // 2, cols // 2)
    (paired,) = exchange([summed], ["pair"], outer, inner, 4)
    reduced = paired.transpose(1, 0, 2).reshape(rows // 2, cols)
    return (grad_in, reduced[:, :qk], reduced[:, qk : 2 * qk], reduced[:, 2 * qk :])


def solution(mesh):
    in_specs = (P("batch", "seq", None), P("batch", "seq", None), P(), P(), P())
    out_specs = (
        P("batch", "seq", None),
        P(("seq", "batch"), None),
        P(("seq", "batch"), None),
        P(("seq", "batch"), None),
    )
    return jax.shard_map(body, mesh=mesh, in_specs=in_specs, out_specs=out_specs, check_vma=False)
```

time: 580 us -> 197 us (0.34)
  the two profiles are of different devices: /device:TPU:0 before, /device:TPU:9 now
where the time goes in v1:
time: 197 us; the launch traced here: 196 us
  Pallas kernels  162 us (82%)
  local copies, waits for them, and re-layouts  17.2 us (9%)
  matrix products  13 us (7%)
  other arithmetic  3.57 us (2%)
    pallas_call x5, Pallas kernels, exchange(): pl.pallas_call(functools.partial(exchange_kernel, kinds, outer, inner), o...  146 us
    pallas_call x1, Pallas kernels, attention(): pl.pallas_call(functools.partial(attention_kernel, wide), out_shape=jax.S...  15.7 us
    dot_general x1, matrix products, body(): lax.dot_general(joined, weights, (((0,), (1,)), ((), ())), preferred_elem...  5.12 us
    concatenate x1, local copies, waits for them, and re-layouts, body(): weights = jnp.concatenate([w_query, w_key, w_value], 1)  4.69 us
    unnamed x9, local copies, waits for them, and re-layouts  4.1 us
    dot_general x1, matrix products, body(): lax.dot_general(weights, tokens, (((0,), (1,)), ((), ())), preferred_elem...  4.05 us

profile of v1, /device:TPU:9, one launch (start us, length us, event | category | flops | bytes accessed | tf_op | source)
XLA Modules:
  0.0 196.4 jit_solution(12140732574786656509)
XLA Ops:
  0.6 1.9 constant_dynamic-update-slice_fusion.2
  2.6 1.9 constant_dynamic-update-slice_fusion.1
  4.5 0.0 copy-start.2
  4.5 0.0 copy-start.1
  4.5 4.7 %constant_dynamic-update-slice_fusion = bf16[2048,1280]{1,0:T(8,128)(2,1)} fusion(bf16[2048,1280]{1,0:T(8,128)(2,1)} %constant_dynamic-update-slice_fusion.1, bf16[2048,1024]{1,0:T(8,128)(2,1)} %param.10), kind=kLoop, calls=%fused_computation.12 | loop fusion | bytes 8388608 | tf_op jit(solution)/shard_map/concatenate | solution.py:247
  9.2 0.0 copy-done.2
  9.2 0.2 copy.28
  9.4 0.0 copy-done.1
  9.4 4.0 %fusion.4 = f32[1280,128]{1,0:T(8,128)S(1)} fusion(bf16[2048,1280]{1,0:T(8,128)(2,1)} %constant_dynamic-update-slice_fusion, bf16[1,128,2048]{2,1,0:T(8,128)(2,1)S(1)} %copy-done.1), kind=kOutput, calls=%fused_computation.10 | convolution fusion | flops 671088640 | bytes 6422528 | tf_op jit(solution)/shard_map/dot_general | solution.py:250
  13.6 1.2 pad_maximum_fusion.refs_0_
  14.8 0.3 copy.29
  15.1 0.1 convert_bitcast_fusion
  15.2 0.1 copy.30
  15.2 0.3 copy.31
  15.6 1.7 broadcast_in_dim.35
  17.2 48.6 %shard_map.93 = (f32[16,160,128]{2,1,0:T(8,128)}, f32[8,128,512]{2,1,0:T(8,128)}) custom-call(f32[16,160,128]{2,1,0:T(8,128)} %pad_maximum_fusion.refs_0_, f32[8,128,512]{2,1,0:T(8,128)} %bitcast.40), custom_call_target="tpu_custom_call" | custom-call | tf_op jit(solution)/shard_map/pallas_call | solution.py:72
  65.9 15.7 %shard_map.94.refs_0_ = f32[16,96,128]{2,1,0:T(8,128)} custom-call(f32[16,160,128]{2,1,0:T(8,128)} %get-tuple-element.6.r_ref, f32[192,128]{1,0:T(8,128)} %constant.4.clone.c_ref), custom_call_target="tpu_custom_call" | custom-call | tf_op jit(solution)/shard_map/pallas_call | solution.py:229
  81.6 23.3 %shard_map.95 = f32[16,96,128]{2,1,0:T(8,128)} custom-call(f32[16,96,128]{2,1,0:T(8,128)} %shard_map.94.refs_0_), custom_call_target="tpu_custom_call" | custom-call | tf_op jit(solution)/shard_map/pallas_call | solution.py:72
  104.9 1.1 slice.44
  106.0 1.0 slice.43
  107.0 5.1 %fusion = bf16[1,128,2048]{2,1,0:T(8,128)(2,1)} fusion(bf16[2048,1280]{1,0:T(8,128)(2,1)} %constant_dynamic-update-slice_fusion, bf16[1024,128]{1,0:T(8,128)(2,1)S(1)} %bitcast.43, bf16[256,128]{1,0:T(8,128)(2,1)S(1)} %bitcast.54), kind=kOutput, calls=%fused_computation.1 | convolution fusion | flops 672006144 | bytes 6094848 | tf_op jit(solution)/shard_map/dot_general | solution.py:267
  112.2 1.7 broadcast_in_dim.37
  113.9 0.0 copy-start
  113.9 37.7 %shard_map.96 = f32[8,640,128]{2,1,0:T(8,128)} custom-call(f32[8,640,128]{2,1,0:T(8,128)} %bitcast.39), custom_call_target="tpu_custom_call" | custom-call | tf_op jit(solution)/shard_map/pallas_call | solution.py:72
  151.5 0.0 copy-done
  151.6 3.9 %fusion.1 = f32[512,640,1]{1,0,2:T(8,128)} fusion(f32[8,640,128]{2,1,0:T(8,128)} %shard_map.96, f32[8,128,512]{2,1,0:T(8,128)S(1)} %copy-done), kind=kOutput, calls=%fused_computation.3 | convolution fusion | flops 672268288 | bytes 6029312 | tf_op jit(solution)/shard_map/gtr,gct->rc/dot_general | solution.py:275
  155.4 33.2 %shard_map.97 = f32[4,128,640]{2,1,0:T(8,128)} custom-call(f32[4,128,640]{2,1,0:T(8,128)} %bitcast.41), custom_call_target="tpu_custom_call" | custom-call | tf_op jit(solution)/shard_map/pallas_call | solution.py:72
  188.6 2.2 %reduce_sum.19 = f32[128,640]{1,0:T(8,128)} reduce(f32[4,128,640]{2,1,0:T(8,128)} %shard_map.97, f32[]{:T(128)} %constant.1.clone.1), dimensions={0}, to_apply=%region_1.0 | reduce | flops 245760 | bytes 1638404 | tf_op jit(solution)/shard_map/reduce_sum | solution.py:279
  190.8 3.3 %shard_map.98 = f32[2,64,640]{2,1,0:T(8,128)} custom-call(f32[2,64,640]{2,1,0:T(8,128)} %bitcast.50), custom_call_target="tpu_custom_call" | custom-call | tf_op jit(solution)/shard_map/pallas_call | solution.py:72
  194.0 1.0 copy.36
  195.0 0.6 fusion.7
  195.7 0.7 slice.53
  (9 shorter events, 0.2 us)
Async XLA Ops:
  4.5 4.7 %copy-start.2 = (bf16[1,128,1024]{2,1,0:T(8,128)(2,1)S(1)}, bf16[1,128,1024]{2,1,0:T(8,128)(2,1)}, u32[]{:S(2)}) copy-start(bf16[1,128,1024]{2,1,0:T(8,128)(2,1)} %param.7) | copy-start | bytes 786436
  4.5 4.9 %copy-start.1 = (bf16[1,128,2048]{2,1,0:T(8,128)(2,1)S(1)}, bf16[1,128,2048]{2,1,0:T(8,128)(2,1)}, u32[]{:S(2)}) copy-start(bf16[1,128,2048]{2,1,0:T(8,128)(2,1)} %param.6) | copy-start | bytes 1572868
  113.9 37.7 %copy-start = (f32[8,128,512]{2,1,0:T(8,128)S(1)}, f32[8,128,512]{2,1,0:T(8,128)}, u32[]{:S(2)}) copy-start(f32[8,128,512]{2,1,0:T(8,128)} %get-tuple-element.7) | copy-start | bytes 6291460

commit v2 on v1

--- a/solution.py
+++ b/solution.py
@@ -29,14 +29,12 @@
         return inner * 2, low * 2 + core, lambda j: (high * inner + j // 2, j % 2)
     if kind == "line":
         return outer, high, lambda j: (j * inner + low, core)
+    if kind == "chips":
+        return inner, low, lambda j: (high * inner + j, core)
     return 2, core, lambda j: (seq, j)
 
 
-def exchange_kernel(kinds, outer, inner, *refs):
-    count = len(kinds)
-    ins, outs = refs[:count], refs[count : 2 * count]
-    sends, recvs = refs[2 * count : 3 * count], refs[3 * count :]
-    groups = [group(kind, outer, inner) for kind in kinds]
+def greet(groups):
     barrier = pltpu.get_barrier_semaphore()
     total = 0
     for size, me, where in groups:
@@ -46,39 +44,56 @@
             )
         total += size - 1
     pl.semaphore_wait(barrier, total)
+
+
+def push(src, dst, send, recv, device):
+    copy = pltpu.make_async_remote_copy(
+        src_ref=src,
+        dst_ref=dst,
+        send_sem=send,
+        recv_sem=recv,
+        device_id=device,
+        device_id_type=MESH,
+    )
+    copy.start()
+    return copy
+
+
+def exchange_kernel(outer, inner, src, dst, send, recv):
+    size, me, where = group("seq", outer, inner)
+    greet([(size, me, where)])
     copies = []
-    for (size, me, where), src, dst, send, recv in zip(groups, ins, outs, sends, recvs):
-        for k in range(1, size):
-            peer = (me + k) % size
-            copy = pltpu.make_async_remote_copy(
-                src_ref=src.at[peer],
-                dst_ref=dst.at[me],
-                send_sem=send.at[k],
-                recv_sem=recv.at[k],
-                device_id=where(peer),
-                device_id_type=MESH,
-            )
-            copy.start()
-            copies.append(copy)
-    for (size, me, where), src, dst in zip(groups, ins, outs):
-        dst[me] = src[me]
+    for k in range(1, size):
+        peer = (me + k) % size
+        copies.append(push(src.at[peer], dst.at[me], send.at[k], recv.at[k], where(peer)))
+    dst[me] = src[me]
     for copy in copies:
         copy.wait()
 
 
-def exchange(arrays, kinds, outer, inner, number):
-    sizes = {"seq": outer * inner, "plane": inner * 2, "line": outer, "pair": 2}
-    sems = [pltpu.SemaphoreType.DMA((sizes[k],)) for k in kinds]
+VMEM = pl.BlockSpec(memory_space=pltpu.VMEM)
+HBM = pl.BlockSpec(memory_space=pl.ANY)
+
+
+def sems(*sizes):
+    return pltpu.SemaphoreType.DMA(sizes)
+
+
+def params(number):
+    return pltpu.CompilerParams(
+        collective_id=number, has_side_effects=True, vmem_limit_bytes=60 << 20
+    )
+
+
+def exchange(array, outer, inner):
     return pl.pallas_call(
-        functools.partial(exchange_kernel, kinds, outer, inner),
-        out_shape=[jax.ShapeDtypeStruct(a.shape, a.dtype) for a in arrays],
-        in_specs=[pl.BlockSpec(memory_space=pltpu.VMEM)] * len(arrays),
-        out_specs=[pl.BlockSpec(memory_space=pltpu.VMEM)] * len(arrays),
-        scratch_shapes=sems + sems,
-        compiler_params=pltpu.CompilerParams(
-            collective_id=number, has_side_effects=True, vmem_limit_bytes=60 << 20
-        ),
-    )(*arrays)
+        functools.partial(exchange_kernel, outer, inner),
+        out_shape=jax.ShapeDtypeStruct(array.shape, array.dtype),
+        in_specs=[VMEM],
+        out_specs=VMEM,
+        scratch_shapes=[sems(outer * inner), sems(outer * inner)],
+        compiler_params=params(1),
+    )(array)
 
 
 def dot(left, right, dims):
@@ -236,50 +251,225 @@
     )(received, jnp.asarray(coef))
 
 
+def front_kernel(
+    outer, inner, x_ref, up_ref, in_ref, wq_hbm, wk_hbm, wv_hbm, out_ref, got_ref,
+    wq_ref, wk_ref, wv_ref, own_ref, load, send_u, recv_u, send_i, recv_i, send_p, recv_p,
+):
+    loads = []
+    for n, (src, dst) in enumerate(((wq_hbm, wq_ref), (wk_hbm, wk_ref), (wv_hbm, wv_ref))):
+        copy = pltpu.make_async_copy(src, dst, load.at[n])
+        copy.start()
+        loads.append(copy)
+    size, me, where = group("seq", outer, inner)
+    chips, low, chip = group("chips", outer, inner)
+    greet([(size, me, where), (chips, low, chip)])
+    split = size // H
+    wide = DV // split
+    cut = 2 * DK + wide
+    copies = []
+    for k in range(1, size):
+        peer = (me + k) % size
+        dst = out_ref.at[me, pl.ds(cut, wide)]
+        copies.append(push(up_ref.at[peer], dst, send_u.at[k], recv_u.at[k], where(peer)))
+    for k in range(1, chips):
+        peer = (low + k) % chips
+        copies.append(
+            push(in_ref.at[peer], got_ref.at[low], send_i.at[k], recv_i.at[k], chip(peer))
+        )
+    x = x_ref[...]
+    for n, (w_ref, copy) in enumerate(zip((wq_ref, wk_ref), loads)):
+        copy.wait()
+        flat = dot(x, w_ref[...], (1, 0)).T
+        for s in range(size):
+            at = (s // split) * DK
+            own_ref[s, n * DK : (n + 1) * DK, :] = flat[at : at + DK]
+    loads[2].wait()
+    for s in range(0, size, DV // wide):
+        at = s * wide
+        flat = dot(x, wv_ref[:, at : at + DV], (1, 0)).astype(BF).astype(F32).T
+        for n in range(DV // wide):
+            own_ref[s + n, 2 * DK :, :] = flat[n * wide : (n + 1) * wide]
+    for k in range(1, size):
+        peer = (me + k) % size
+        dst = out_ref.at[me, pl.ds(0, cut)]
+        copies.append(push(own_ref.at[peer], dst, send_p.at[k], recv_p.at[k], where(peer)))
+    out_ref[me, :cut, :] = own_ref[me]
+    out_ref[me, cut:, :] = up_ref[me]
+    got_ref[low] = in_ref[low]
+    for copy in copies:
+        copy.wait()
+
+
+def front(tokens, upstream, staged, weights, outer, inner):
+    seqs, wide, length = upstream.shape
+    cut = 2 * DK + wide
+    w_scratch = [pltpu.VMEM(w.shape, w.dtype) for w in weights]
+    pairs = [sems(seqs), sems(seqs), sems(inner), sems(inner), sems(seqs), sems(seqs)]
+    return pl.pallas_call(
+        functools.partial(front_kernel, outer, inner),
+        out_shape=[
+            jax.ShapeDtypeStruct((seqs, cut + wide, length), F32),
+            jax.ShapeDtypeStruct(staged.shape, F32),
+        ],
+        in_specs=[VMEM] * 3 + [HBM] * 3,
+        out_specs=[VMEM] * 2,
+        scratch_shapes=w_scratch + [pltpu.VMEM((seqs, cut, length), F32), sems(3)] + pairs,
+        compiler_params=params(0),
+    )(tokens, upstream, staged, *weights)
+
+
+def tail_kernel(
+    outer, inner, pieces, g_ref, in_ref, wq_hbm, wk_hbm, wv_hbm, gi_ref, o_ref,
+    wq_ref, wk_ref, wv_ref, jt_ref, jb_ref, gj_ref, pg_ref, xb_ref, ls_ref, lr_ref, fs_ref, os_ref,
+    load, send_x, recv_x, send_j, recv_j, send_l, recv_l, send_o, recv_o,
+):
+    loads = []
+    for n, (src, dst) in enumerate(((wq_hbm, wq_ref), (wk_hbm, wk_ref), (wv_hbm, wv_ref))):
+        copy = pltpu.make_async_copy(src, dst, load.at[n])
+        copy.start()
+        loads.append(copy)
+    plane, mine, where = group("plane", outer, inner)
+    lines, high, along = group("line", outer, inner)
+    _, core, sibling = group("pair", outer, inner)
+    greet([(plane, mine, where), (lines, high, along), (2, core, sibling)])
+    other = 1 - core
+    pending = [push(in_ref, pg_ref, send_x.at[0], recv_x.at[0], sibling(other))]
+    seqs = outer * inner
+    split = seqs // H
+    wide = DV // split
+    blocks = []
+    for n in range(2):
+        rows = []
+        for h in range(H):
+            total = g_ref[h * split, n * DK : (n + 1) * DK, :]
+            for s in range(1, split):
+                total = total + g_ref[h * split + s, n * DK : (n + 1) * DK, :]
+            rows.append(total)
+        blocks.append(jnp.concatenate(rows, 0))
+    for h in range(H):
+        blocks.append(
+            jnp.concatenate([g_ref[h * split + s, 2 * DK :, :] for s in range(split)], 0)
+        )
+    for i in range(pieces):
+        for half in range(2):
+            jb_ref[half, i] = blocks[half * pieces + i].astype(BF).astype(F32)
+    gathers = []
+    for i in range(pieces):
+        row = []
+        for k in range(1, plane):
+            peer = (mine + k) % plane
+            src = jb_ref.at[peer % 2, i]
+            row.append(
+                push(src, gj_ref.at[i, mine], send_j.at[i, k], recv_j.at[i, k], where(peer))
+            )
+        gathers.append(row)
+    for n, block in enumerate(blocks):
+        jt_ref[:, n * DV : (n + 1) * DV] = block.T.astype(BF)
+    for i in range(pieces):
+        gj_ref[i, mine] = jb_ref[core, i]
+    for j in range(inner):
+        xb_ref[2 * j + core] = in_ref[j].astype(BF)
+    for copy in loads:
+        copy.wait()
+    depth = gi_ref.shape[1] // pieces // 256 * 256
+    starts = [i * depth for i in range(pieces)] + [gi_ref.shape[1]]
+    pending[0].wait()
+    for j in range(inner):
+        xb_ref[2 * j + other] = pg_ref[j].astype(BF)
+    tokens = plane * in_ref.shape[1]
+    rows = in_ref.shape[2] // lines
+    reduces = []
+    for i in range(pieces):
+        cut = slice(starts[i], starts[i + 1])
+        total = dot(jt_ref[:, :DV], wq_ref[cut, :], (1, 1))
+        total = total + dot(jt_ref[:, DV : 2 * DV], wk_ref[cut, :], (1, 1))
+        total = total + dot(jt_ref[:, 2 * DV :], wv_ref[cut, :], (1, 1))
+        gi_ref[:, cut] = total.astype(BF)
+        for copy in gathers[i]:
+            copy.wait_recv()
+        grads = jnp.concatenate([gj_ref[i, j].astype(BF) for j in range(plane)], 1)
+        part = dot(grads, xb_ref[...].reshape(tokens, in_ref.shape[2]), (1, 0))
+        for z in range(lines):
+            ls_ref[i, z] = part[:, z * rows : (z + 1) * rows]
+        row = []
+        for k in range(1, lines):
+            peer = (high + k) % lines
+            row.append(
+                push(ls_ref.at[i, peer], lr_ref.at[i, k], send_l.at[i, k], recv_l.at[i, k], along(peer))
+            )
+        reduces.append(row)
+    lasts = []
+    keep = rows // 2
+    for i in range(pieces):
+        total = ls_ref[i, high]
+        for k, copy in enumerate(reduces[i]):
+            copy.wait_recv()
+            total = total + lr_ref[i, k + 1]
+        fs_ref[i] = total.T
+        src = fs_ref.at[i, pl.ds(pl.multiple_of(other * keep, keep), keep)]
+        lasts.append(push(src, os_ref.at[i], send_o.at[i], recv_o.at[i], sibling(other)))
+        o_ref[core * pieces + i] = fs_ref[i, pl.ds(pl.multiple_of(core * keep, keep), keep), :]
+    for i, copy in enumerate(lasts):
+        copy.wait_recv()
+        o_ref[other * pieces + i] = os_ref[i]
+    for row in gathers + reduces + [lasts]:
+        for copy in row:
+            copy.wait_send()
+
+
+def tail(grads, inside, weights, outer, inner):
+    seqs, _, length = grads.shape
+    width = weights[0].shape[0]
+    pieces = sum(w.shape[1] for w in weights) // (2 * DV)
+    rows = width // seqs
+    plane = 2 * inner
+    vm = lambda *shape: pltpu.VMEM(shape, F32)
+    scratch = [pltpu.VMEM(w.shape, w.dtype) for w in weights] + [
+        pltpu.VMEM((length, 2 * pieces * DV), BF),
+        vm(2, pieces, DV, length),
+        vm(pieces, plane, DV, length),
+        vm(inner, length, outer * rows),
+        pltpu.VMEM((plane, length, outer * rows), BF),
+        vm(pieces, outer, DV, rows),
+        vm(pieces, outer, DV, rows),
+        vm(pieces, rows, DV),
+        vm(pieces, rows // 2, DV),
+        sems(3), sems(1), sems(1),
+        sems(pieces, plane), sems(pieces, plane),
+        sems(pieces, outer), sems(pieces, outer),
+        sems(pieces), sems(pieces),
+    ]
+    return pl.pallas_call(
+        functools.partial(tail_kernel, outer, inner, pieces),
+        out_shape=[
+            jax.ShapeDtypeStruct((length, width), BF),
+            jax.ShapeDtypeStruct((2 * pieces, rows // 2, DV), F32),
+        ],
+        in_specs=[VMEM] * 2 + [HBM] * 3,
+        out_specs=[VMEM] * 2,
+        scratch_shapes=scratch,
+        compiler_params=params(2),
+    )(grads, inside, *weights)
+
+
 def body(inputs, cotangent, w_query, w_key, w_value):
     seqs = lax.axis_size("seq")
     outer = 4 if seqs % 4 == 0 else 1
     inner = seqs // outer
-    split = seqs // H
-    wide = DV // split
+    wide = DV * H // seqs
     tokens = inputs[0]
     length, width = tokens.shape
-    weights = jnp.concatenate([w_query, w_key, w_value], 1)
-    cols = weights.shape[1]
-    qk = H * DK
-    proj = lax.dot_general(weights, tokens, (((0,), (1,)), ((), ())), preferred_element_type=F32)
-    heads = proj[: 2 * qk].reshape(2, H, 1, DK, length)
-    heads = jnp.broadcast_to(heads, (2, H, split, DK, length)).reshape(2, seqs, DK, length)
-    values = proj[2 * qk :].astype(BF).astype(F32).reshape(seqs, wide, length)
+    weights = (w_query, w_key, w_value)
     upstream = cotangent[0].astype(F32).T.reshape(seqs, wide, length)
-    sent = jnp.concatenate([heads[0], heads[1], values, upstream], 1)
     rows = width // seqs
     staged = tokens.astype(F32).reshape(length, outer, inner, rows).transpose(2, 0, 1, 3)
-    staged = staged.reshape(inner, 1, length, outer * rows)
-    staged = jnp.broadcast_to(staged, (inner, 2, length, outer * rows))
-    staged = staged.reshape(inner * 2, length, outer * rows)
-    received, group_in = exchange([sent, staged], ["seq", "plane"], outer, inner, 0)
+    staged = staged.reshape(inner, length, outer * rows)
+    received, inside = front(tokens, upstream, staged, weights, outer, inner)
     back = attention(received, wide)
-    (grads,) = exchange([back], ["seq"], outer, inner, 1)
-    small = grads[:, : 2 * DK].reshape(H, split, 2, DK, length).sum(1)
-    small = small.transpose(1, 0, 2, 3).reshape(2 * qk, length)
-    joined = jnp.concatenate([small, grads[:, 2 * DK :].reshape(H * DV, length)], 0).astype(BF)
-    grad_in = lax.dot_general(
-        joined, weights, (((0,), (1,)), ((), ())), preferred_element_type=F32
-    ).astype(BF)[None]
-    part = joined.astype(F32).reshape(1, 2, cols // 2, length)
-    part = jnp.broadcast_to(part, (inner, 2, cols // 2, length)).reshape(
-        inner * 2, cols // 2, length
-    )
-    (group_grad,) = exchange([part], ["plane"], outer, inner, 2)
-    partial = jnp.einsum(
-        "gtr,gct->rc", group_in.astype(BF), group_grad.astype(BF), preferred_element_type=F32
-    )
-    (lined,) = exchange([partial.reshape(outer, rows, cols // 2)], ["line"], outer, inner, 3)
-    summed = lined.sum(0).reshape(2, rows // 2, cols // 2)
-    (paired,) = exchange([summed], ["pair"], outer, inner, 4)
-    reduced = paired.transpose(1, 0, 2).reshape(rows // 2, cols)
-    return (grad_in, reduced[:, :qk], reduced[:, qk : 2 * qk], reduced[:, 2 * qk :])
+    grads = exchange(back, outer, inner)
+    grad_in, blocks = tail(grads, inside, weights, outer, inner)
+    grad_wv = blocks[2:].transpose(1, 0, 2).reshape(rows // 2, H * DV)
+    return (grad_in[None], blocks[0], blocks[1], grad_wv)
 
 
 def solution(mesh):

time: 197 us -> 134 us (0.68)
  the two profiles are of different devices: /device:TPU:9 before, /device:TPU:0 now
where the time goes in v2:
time: 134 us; the launch traced here: 133 us
  Pallas kernels  122 us (91%)
  local copies, waits for them, and re-layouts  9.5 us (7%)
    pallas_call x1, Pallas kernels, tail(): pl.pallas_call(functools.partial(tail_kernel, outer, inner, pieces), out_...  48.8 us
    pallas_call x1, Pallas kernels, front(): pl.pallas_call(functools.partial(front_kernel, outer, inner), out_shape=[...  37.4 us
    pallas_call x1, Pallas kernels, exchange(): pl.pallas_call(functools.partial(exchange_kernel, outer, inner), out_shap...  20.3 us
    pallas_call x1, Pallas kernels, attention(): pl.pallas_call(functools.partial(attention_kernel, wide), out_shape=jax.S...  15.7 us
    reshape x3, local copies, waits for them, and re-layouts, body(): staged = staged.reshape(inner, length, outer * rows)  3.55 us

profile of v2, /device:TPU:0, one launch (start us, length us, event | category | flops | bytes accessed | tf_op | source)
XLA Modules:
  0.0 133.5 jit_solution(2850835276339189458)
XLA Ops:
  0.6 1.0 convert_bitcast_fusion
  1.6 1.0 copy.12
  2.6 1.9 %reshape.41 = f32[128,4,4,128]{3,2,1,0:T(4,128)S(1)} reshape(bf16[1,128,2048]{2,1,0:T(8,128)(2,1)} %param.6) | data formatting | bytes 1572864 | tf_op jit(solution)/shard_map/reshape | solution.py:466
  4.5 0.3 copy.18
  4.8 1.4 %reshape.35.in_ref = f32[4,128,512]{2,1,0:T(8,128)} reshape(f32[4,128,4,128]{3,2,1,0:T(4,128)S(1)} %bitcast.21) | data formatting | bytes 2097152 | tf_op jit(solution)/shard_map/reshape | solution.py:466
  6.2 37.4 %shard_map.93 = (f32[16,160,128]{2,1,0:T(8,128)}, f32[4,128,512]{2,1,0:T(8,128)}) custom-call(bf16[128,2048]{1,0:T(8,128)(2,1)} %bitcast.22, f32[16,64,128]{2,1,0:T(8,128)} %bitcast.23, f32[4,128,512]{2,1,0:T(8,128)} %reshape.35.in_ref, bf16[2048,128]{1,0:T(8,128)(2,1)} %wq_hbm.3, bf16[2048,128]{1,0:T(8,128)(2,1)} %wk_hbm.3, bf16[2048,1024]{1,0:T(8,128)(2,1)} %wv_hbm.3), custom_call_target="tpu_custom_call" | custom-call | tf_op jit(solution)/shard_map/pallas_call | solution.py:308
  43.6 15.7 %shard_map.94.src = f32[16,96,128]{2,1,0:T(8,128)} custom-call(f32[16,160,128]{2,1,0:T(8,128)} %get-tuple-element.8.r_ref, f32[192,128]{1,0:T(8,128)} %constant.2.clone.c_ref), custom_call_target="tpu_custom_call" | custom-call | tf_op jit(solution)/shard_map/pallas_call | solution.py:244
  59.3 20.3 %shard_map.95.g_ref = f32[16,96,128]{2,1,0:T(8,128)} custom-call(f32[16,96,128]{2,1,0:T(8,128)} %shard_map.94.src), custom_call_target="tpu_custom_call" | custom-call | tf_op jit(solution)/shard_map/pallas_call | solution.py:89
  79.7 48.8 %shard_map.96 = (bf16[128,2048]{1,0:T(8,128)(2,1)}, f32[10,64,128]{2,1,0:T(8,128)}) custom-call(f32[16,96,128]{2,1,0:T(8,128)} %shard_map.95.g_ref, f32[4,128,512]{2,1,0:T(8,128)} %get-tuple-element.9.in_ref, bf16[2048,128]{1,0:T(8,128)(2,1)} %wq_hbm.3, bf16[2048,128]{1,0:T(8,128)(2,1)} %wk_hbm.3, bf16[2048,1024]{1,0:T(8,128)(2,1)} %wv_hbm.3), custom_call_target="tpu_custom_call" | custom-call | tf_op jit(solution)/shard_map/pallas_call | solution.py:442
  128.5 1.4 %slice_bitcast_fusion.1 = (f32[64,128]{1,0:T(8,128)}, f32[64,128]{1,0:T(8,128)}) fusion(f32[10,64,128]{2,1,0:T(8,128)} %get-tuple-element.11), kind=kLoop, calls=%fused_computation.4 | loop fusion | bytes 131072 | tf_op jit(solution)/shard_map/squeeze | solution.py:472
  129.9 1.7 %copy_bitcast_fusion.1 = f32[64,1024]{1,0:T(8,128)} fusion(f32[10,64,128]{2,1,0:T(8,128)} %get-tuple-element.11), kind=kLoop, calls=%fused_computation.2 | loop fusion | bytes 524288 | tf_op jit(solution)/shard_map/reshape | solution.py:471
  131.6 1.9 %copy.20 = bf16[1,128,2048]{2,1,0:T(8,128)(2,1)} copy(bf16[1,128,2048]{2,1,0:T(8,128)(2,1)} %bitcast.24) | data formatting | bytes 1048576

commit v3 on v2

--- a/solution.py
+++ b/solution.py
@@ -59,18 +59,6 @@
     return copy
 
 
-def exchange_kernel(outer, inner, src, dst, send, recv):
-    size, me, where = group("seq", outer, inner)
-    greet([(size, me, where)])
-    copies = []
-    for k in range(1, size):
-        peer = (me + k) % size
-        copies.append(push(src.at[peer], dst.at[me], send.at[k], recv.at[k], where(peer)))
-    dst[me] = src[me]
-    for copy in copies:
-        copy.wait()
-
-
 VMEM = pl.BlockSpec(memory_space=pltpu.VMEM)
 HBM = pl.BlockSpec(memory_space=pl.ANY)
 
@@ -83,17 +71,6 @@
     return pltpu.CompilerParams(
         collective_id=number, has_side_effects=True, vmem_limit_bytes=60 << 20
     )
-
-
-def exchange(array, outer, inner):
-    return pl.pallas_call(
-        functools.partial(exchange_kernel, outer, inner),
-        out_shape=jax.ShapeDtypeStruct(array.shape, array.dtype),
-        in_specs=[VMEM],
-        out_specs=VMEM,
-        scratch_shapes=[sems(outer * inner), sems(outer * inner)],
-        compiler_params=params(1),
-    )(array)
 
 
 def dot(left, right, dims):
@@ -164,8 +141,28 @@
     return total + jnp.concatenate([jnp.zeros_like(lower), lower], 0)
 
 
-def attention_kernel(wide, r_ref, c_ref, o_ref, fq_ref, fk_ref, va_ref, ah, al, gh, gl, nh, nl):
+def attention_kernel(
+    wide, outer, inner, r_ref, c_ref, x_ref, got_ref, xb_ref,
+    o_ref, fq_ref, fk_ref, va_ref, ah, al, gh, gl, nh, nl, st_ref, gi_ref, pg_ref,
+    send_i, recv_i, send_x, recv_x, send_r, recv_r,
+):
     blocks, _, tokens = r_ref.shape
+    size, me, where = group("seq", outer, inner)
+    chips, low, chip = group("chips", outer, inner)
+    _, core, sibling = group("pair", outer, inner)
+    rows = st_ref.shape[2] // outer
+    for j in range(inner):
+        for z in range(outer):
+            at = (z * inner + j) * rows
+            st_ref[j, :, z * rows : (z + 1) * rows] = x_ref[:, at : at + rows].astype(F32)
+    greet([(size, me, where), (chips, low, chip), (2, core, sibling)])
+    inside = []
+    for k in range(1, chips):
+        peer = (low + k) % chips
+        inside.append(
+            push(st_ref.at[peer], gi_ref.at[low], send_i.at[k], recv_i.at[k], chip(peer))
+        )
+    gi_ref[low] = st_ref[low]
     length = 2 * tokens
     chunks = blocks // 2
     feats = fq_ref.shape[1]
@@ -228,32 +225,67 @@
         store(c, 2 * DK, gv[:wide])
         gfk = dot2r(fq, ga, (1, 1)) + dot2(held, va, (0, 0))
         store(c, DK, pull(uk, gfk, coef) * 0.5)
+        for t in range(2):
+            peer = 2 * c + t
+
+            @pl.when(peer != me)
+            def _():
+                push(o_ref.at[peer], got_ref.at[me], send_r.at[peer], recv_r.at[me], where(peer))
+
         return state + dot2(gn, fq, (1, 1))
 
     lax.fori_loop(0, chunks, backward, zero)
-
-
-def attention(received, wide):
+    got_ref[me] = o_ref[me]
+    for copy in inside:
+        copy.wait()
+    pair = push(gi_ref, pg_ref, send_x.at[0], recv_x.at[0], sibling(1 - core))
+    for j in range(inner):
+        xb_ref[2 * j + core] = gi_ref[j].astype(BF)
+    pair.wait()
+    for j in range(inner):
+        xb_ref[2 * j + 1 - core] = pg_ref[j].astype(BF)
+    for k in range(1, size):
+        peer = (me + k) % size
+        pltpu.make_async_remote_copy(
+            src_ref=o_ref.at[peer],
+            dst_ref=got_ref.at[peer],
+            send_sem=send_r.at[peer],
+            recv_sem=recv_r.at[peer],
+            device_id=where(peer),
+            device_id_type=MESH,
+        ).wait()
+
+
+def attention(received, tokens_in, wide, outer, inner):
     blocks, _, tokens = received.shape
     coef = coefs()
     feats = coef.shape[0] + DK + AUX
     chunks, length = blocks // 2, 2 * tokens
+    width = tokens_in.shape[1] // inner
     square = pltpu.VMEM((chunks, length, length), BF)
     grads = pltpu.VMEM((chunks, wide + AUX, length), BF)
     feat = pltpu.VMEM((chunks, feats, length), BF)
+    result = (blocks, 2 * DK + wide, tokens)
+    group_in = pltpu.VMEM((inner, tokens, width), F32)
+    scratch = [pltpu.VMEM(result, F32), feat, feat, grads, square, square, square, square]
+    scratch += [grads, grads, group_in, group_in, group_in]
+    scratch += [sems(inner)] * 2 + [sems(1)] * 2 + [sems(blocks)] * 2
     return pl.pallas_call(
-        functools.partial(attention_kernel, wide),
-        out_shape=jax.ShapeDtypeStruct((blocks, 2 * DK + wide, tokens), F32),
-        in_specs=[pl.BlockSpec(memory_space=pltpu.VMEM)] * 2,
-        out_specs=pl.BlockSpec(memory_space=pltpu.VMEM),
-        scratch_shapes=[feat, feat, grads, square, square, square, square, grads, grads],
-        compiler_params=pltpu.CompilerParams(vmem_limit_bytes=60 << 20),
-    )(received, jnp.asarray(coef))
+        functools.partial(attention_kernel, wide, outer, inner),
+        out_shape=[
+            jax.ShapeDtypeStruct(result, F32),
+            jax.ShapeDtypeStruct((2 * inner, tokens, width), BF),
+        ],
+        in_specs=[VMEM] * 3,
+        out_specs=[VMEM] * 2,
+        scratch_shapes=scratch,
+        compiler_params=params(1),
+    )(received, jnp.asarray(coef), tokens_in)
 
 
 def front_kernel(
-    outer, inner, x_ref, up_ref, in_ref, wq_hbm, wk_hbm, wv_hbm, out_ref, got_ref,
-    wq_ref, wk_ref, wv_ref, own_ref, load, send_u, recv_u, send_i, recv_i, send_p, recv_p,
+    outer, inner, x_ref, c_ref, wq_hbm, wk_hbm, wv_hbm, out_ref,
+    wq_ref, wk_ref, wv_ref, own_ref, up_ref, load, send_u, recv_u, send_p, recv_p,
 ):
     loads = []
     for n, (src, dst) in enumerate(((wq_hbm, wq_ref), (wk_hbm, wk_ref), (wv_hbm, wv_ref))):
@@ -261,21 +293,19 @@
         copy.start()
         loads.append(copy)
     size, me, where = group("seq", outer, inner)
-    chips, low, chip = group("chips", outer, inner)
-    greet([(size, me, where), (chips, low, chip)])
     split = size // H
     wide = DV // split
     cut = 2 * DK + wide
+    for h in range(H):
+        flat = c_ref[:, h * DV : (h + 1) * DV].astype(F32).T
+        for n in range(split):
+            up_ref[h * split + n] = flat[n * wide : (n + 1) * wide]
+    greet([(size, me, where)])
     copies = []
     for k in range(1, size):
         peer = (me + k) % size
         dst = out_ref.at[me, pl.ds(cut, wide)]
         copies.append(push(up_ref.at[peer], dst, send_u.at[k], recv_u.at[k], where(peer)))
-    for k in range(1, chips):
-        peer = (low + k) % chips
-        copies.append(
-            push(in_ref.at[peer], got_ref.at[low], send_i.at[k], recv_i.at[k], chip(peer))
-        )
     x = x_ref[...]
     for n, (w_ref, copy) in enumerate(zip((wq_ref, wk_ref), loads)):
         copy.wait()
@@ -284,44 +314,41 @@
             at = (s // split) * DK
             own_ref[s, n * DK : (n + 1) * DK, :] = flat[at : at + DK]
     loads[2].wait()
-    for s in range(0, size, DV // wide):
-        at = s * wide
-        flat = dot(x, wv_ref[:, at : at + DV], (1, 0)).astype(BF).astype(F32).T
-        for n in range(DV // wide):
-            own_ref[s + n, 2 * DK :, :] = flat[n * wide : (n + 1) * wide]
+    for h in range(H):
+        flat = dot(x, wv_ref[:, h * DV : (h + 1) * DV], (1, 0)).astype(BF).astype(F32).T
+        for n in range(split):
+            own_ref[h * split + n, 2 * DK :, :] = flat[n * wide : (n + 1) * wide]
     for k in range(1, size):
         peer = (me + k) % size
         dst = out_ref.at[me, pl.ds(0, cut)]
         copies.append(push(own_ref.at[peer], dst, send_p.at[k], recv_p.at[k], where(peer)))
     out_ref[me, :cut, :] = own_ref[me]
     out_ref[me, cut:, :] = up_ref[me]
-    got_ref[low] = in_ref[low]
     for copy in copies:
         copy.wait()
 
 
-def front(tokens, upstream, staged, weights, outer, inner):
-    seqs, wide, length = upstream.shape
+def front(tokens, upstream, weights, outer, inner):
+    seqs = outer * inner
+    length = tokens.shape[0]
+    wide = DV * H // seqs
     cut = 2 * DK + wide
-    w_scratch = [pltpu.VMEM(w.shape, w.dtype) for w in weights]
-    pairs = [sems(seqs), sems(seqs), sems(inner), sems(inner), sems(seqs), sems(seqs)]
+    scratch = [pltpu.VMEM(w.shape, w.dtype) for w in weights]
+    scratch += [pltpu.VMEM((seqs, cut, length), F32), pltpu.VMEM((seqs, wide, length), F32)]
     return pl.pallas_call(
         functools.partial(front_kernel, outer, inner),
-        out_shape=[
-            jax.ShapeDtypeStruct((seqs, cut + wide, length), F32),
-            jax.ShapeDtypeStruct(staged.shape, F32),
-        ],
-        in_specs=[VMEM] * 3 + [HBM] * 3,
-        out_specs=[VMEM] * 2,
-        scratch_shapes=w_scratch + [pltpu.VMEM((seqs, cut, length), F32), sems(3)] + pairs,
+        out_shape=jax.ShapeDtypeStruct((seqs, cut + wide, length), F32),
+        in_specs=[VMEM] * 2 + [HBM] * 3,
+        out_specs=VMEM,
+        scratch_shapes=scratch + [sems(3)] + [sems(seqs)] * 4,
         compiler_params=params(0),
-    )(tokens, upstream, staged, *weights)
+    )(tokens, upstream, *weights)
 
 
 def tail_kernel(
-    outer, inner, pieces, g_ref, in_ref, wq_hbm, wk_hbm, wv_hbm, gi_ref, o_ref,
-    wq_ref, wk_ref, wv_ref, jt_ref, jb_ref, gj_ref, pg_ref, xb_ref, ls_ref, lr_ref, fs_ref, os_ref,
-    load, send_x, recv_x, send_j, recv_j, send_l, recv_l, send_o, recv_o,
+    outer, inner, pieces, g_ref, xb_ref, wq_hbm, wk_hbm, wv_hbm, gi_ref, oq_ref, ok_ref, ov_ref,
+    wq_ref, wk_ref, wv_ref, jt_ref, jb_ref, gj_ref, ls_ref, lr_ref, fs_ref, os_ref, o_ref,
+    load, send_j, recv_j, send_l, recv_l, send_o, recv_o,
 ):
     loads = []
     for n, (src, dst) in enumerate(((wq_hbm, wq_ref), (wk_hbm, wk_ref), (wv_hbm, wv_ref))):
@@ -333,7 +360,6 @@
     _, core, sibling = group("pair", outer, inner)
     greet([(plane, mine, where), (lines, high, along), (2, core, sibling)])
     other = 1 - core
-    pending = [push(in_ref, pg_ref, send_x.at[0], recv_x.at[0], sibling(other))]
     seqs = outer * inner
     split = seqs // H
     wide = DV // split
@@ -367,17 +393,12 @@
         jt_ref[:, n * DV : (n + 1) * DV] = block.T.astype(BF)
     for i in range(pieces):
         gj_ref[i, mine] = jb_ref[core, i]
-    for j in range(inner):
-        xb_ref[2 * j + core] = in_ref[j].astype(BF)
     for copy in loads:
         copy.wait()
     depth = gi_ref.shape[1] // pieces // 256 * 256
     starts = [i * depth for i in range(pieces)] + [gi_ref.shape[1]]
-    pending[0].wait()
-    for j in range(inner):
-        xb_ref[2 * j + other] = pg_ref[j].astype(BF)
-    tokens = plane * in_ref.shape[1]
-    rows = in_ref.shape[2] // lines
+    tokens = plane * xb_ref.shape[1]
+    rows = xb_ref.shape[2] // lines
     reduces = []
     for i in range(pieces):
         cut = slice(starts[i], starts[i + 1])
@@ -388,7 +409,7 @@
         for copy in gathers[i]:
             copy.wait_recv()
         grads = jnp.concatenate([gj_ref[i, j].astype(BF) for j in range(plane)], 1)
-        part = dot(grads, xb_ref[...].reshape(tokens, in_ref.shape[2]), (1, 0))
+        part = dot(grads, xb_ref[...].reshape(tokens, xb_ref.shape[2]), (1, 0))
         for z in range(lines):
             ls_ref[i, z] = part[:, z * rows : (z + 1) * rows]
         row = []
@@ -412,6 +433,10 @@
     for i, copy in enumerate(lasts):
         copy.wait_recv()
         o_ref[other * pieces + i] = os_ref[i]
+    oq_ref[...] = o_ref[0]
+    ok_ref[...] = o_ref[1]
+    for n in range(H):
+        ov_ref[:, n * DV : (n + 1) * DV] = o_ref[2 + n]
     for row in gathers + reduces + [lasts]:
         for copy in row:
             copy.wait_send()
@@ -428,13 +453,12 @@
         pltpu.VMEM((length, 2 * pieces * DV), BF),
         vm(2, pieces, DV, length),
         vm(pieces, plane, DV, length),
-        vm(inner, length, outer * rows),
-        pltpu.VMEM((plane, length, outer * rows), BF),
         vm(pieces, outer, DV, rows),
         vm(pieces, outer, DV, rows),
         vm(pieces, rows, DV),
         vm(pieces, rows // 2, DV),
-        sems(3), sems(1), sems(1),
+        vm(2 * pieces, rows // 2, DV),
+        sems(3),
         sems(pieces, plane), sems(pieces, plane),
         sems(pieces, outer), sems(pieces, outer),
         sems(pieces), sems(pieces),
@@ -443,10 +467,12 @@
         functools.partial(tail_kernel, outer, inner, pieces),
         out_shape=[
             jax.ShapeDtypeStruct((length, width), BF),
-            jax.ShapeDtypeStruct((2 * pieces, rows // 2, DV), F32),
+            jax.ShapeDtypeStruct((rows // 2, DV), F32),
+            jax.ShapeDtypeStruct((rows // 2, DV), F32),
+            jax.ShapeDtypeStruct((rows // 2, H * DV), F32),
         ],
         in_specs=[VMEM] * 2 + [HBM] * 3,
-        out_specs=[VMEM] * 2,
+        out_specs=[VMEM] * 4,
         scratch_shapes=scratch,
         compiler_params=params(2),
     )(grads, inside, *weights)
@@ -458,18 +484,11 @@
     inner = seqs // outer
     wide = DV * H // seqs
     tokens = inputs[0]
-    length, width = tokens.shape
     weights = (w_query, w_key, w_value)
-    upstream = cotangent[0].astype(F32).T.reshape(seqs, wide, length)
-    rows = width // seqs
-    staged = tokens.astype(F32).reshape(length, outer, inner, rows).transpose(2, 0, 1, 3)
-    staged = staged.reshape(inner, length, outer * rows)
-    received, inside = front(tokens, upstream, staged, weights, outer, inner)
-    back = attention(received, wide)
-    grads = exchange(back, outer, inner)
-    grad_in, blocks = tail(grads, inside, weights, outer, inner)
-    grad_wv = blocks[2:].transpose(1, 0, 2).reshape(rows // 2, H * DV)
-    return (grad_in[None], blocks[0], blocks[1], grad_wv)
+    received = front(tokens, cotangent[0], weights, outer, inner)
+    grads, inside = attention(received, tokens, wide, outer, inner)
+    grad_in, grad_wq, grad_wk, grad_wv = tail(grads, inside, weights, outer, inner)
+    return (grad_in[None], grad_wq, grad_wk, grad_wv)
 
 
 def solution(mesh):

time: 134 us -> 127 us (0.948)
  local copies, waits for them, and re-layouts: 9.5 us -> 6.3 us
  Pallas kernels: 122 us -> 120 us
    reshape x5 -> x0, local copies, waits for them, and re-layouts: 6.22 us -> none  [the longest x3 3.55 us: body(): staged = staged.reshape(inner, length, outer * rows)]
    pallas_call x1, Pallas kernels: 48.8 us -> 44 us  [tail(): pl.pallas_call(functools.partial(tail_kernel, outer, inner, pieces), out_...]
    unnamed x1 -> x4, local copies, waits for them, and re-layouts: 1.88 us -> 6.3 us
    pallas_call x3 -> x2, Pallas kernels: 73.5 us -> 75.6 us  [the longest x1 43 us: attention(): pl.pallas_call(functools.partial(attention_kernel, wide, outer, inner), o...]
    squeeze x1 -> x0, local copies, waits for them, and re-layouts: 1.4 us -> none  [body(): return (grad_in[None], blocks[0], blocks[1], grad_wv)]
where the time goes in v3:
time: 127 us
  Pallas kernels  120 us (94%)
  local copies, waits for them, and re-layouts  6.3 us (5%)
    pallas_call x1, Pallas kernels, tail(): pl.pallas_call(functools.partial(tail_kernel, outer, inner, pieces), out_...  44 us
    pallas_call x1, Pallas kernels, attention(): pl.pallas_call(functools.partial(attention_kernel, wide, outer, inner), o...  43 us
    pallas_call x1, Pallas kernels, front(): pl.pallas_call(functools.partial(front_kernel, outer, inner), out_shape=j...  32.6 us
    unnamed x4, local copies, waits for them, and re-layouts  6.3 us

profile of v3, /device:TPU:0, one launch (start us, length us, event | category | flops | bytes accessed | tf_op | source)
XLA Modules:
  0.0 126.6 jit_solution(5159249258343712834)
XLA Ops:
  0.6 32.6 %shard_map.93.r_ref = f32[16,160,128]{2,1,0:T(8,128)} custom-call(bf16[128,2048]{1,0:T(8,128)(2,1)} %bitcast.3, bf16[128,1024]{1,0:T(8,128)(2,1)} %bitcast.6, bf16[2048,128]{1,0:T(8,128)(2,1)} %wq_hbm.3, bf16[2048,128]{1,0:T(8,128)(2,1)} %wk_hbm.3, bf16[2048,1024]{1,0:T(8,128)(2,1)} %wv_hbm.3), custom_call_target="tpu_custom_call" | custom-call | tf_op jit(solution)/shard_map/pallas_call | solution.py:338
  33.3 43.0 %shard_map.94 = (f32[16,96,128]{2,1,0:T(8,128)}, bf16[8,128,512]{2,1,0:T(8,128)(2,1)}) custom-call(f32[16,160,128]{2,1,0:T(8,128)} %shard_map.93.r_ref, f32[192,128]{1,0:T(8,128)} %constant.2.clone.c_ref, bf16[128,2048]{1,0:T(8,128)(2,1)} %bitcast.4), custom_call_target="tpu_custom_call" | custom-call | tf_op jit(solution)/shard_map/pallas_call | solution.py:273
  76.3 44.0 %shard_map.95 = (bf16[128,2048]{1,0:T(8,128)(2,1)}, f32[64,128]{1,0:T(8,128)}, f32[64,128]{1,0:T(8,128)}, f32[64,1024]{1,0:T(8,128)}) custom-call(f32[16,96,128]{2,1,0:T(8,128)} %get-tuple-element.10.g_ref, bf16[8,128,512]{2,1,0:T(8,128)(2,1)} %get-tuple-element.11.xb_ref, bf16[2048,128]{1,0:T(8,128)(2,1)} %wq_hbm.3, bf16[2048,128]{1,0:T(8,128)(2,1)} %wk_hbm.3, ...), custom_call_target="tpu_custom_call" | custom-call | tf_op jit(solution)/shard_map/pallas_call | solution.py:466
  120.3 1.9 %copy.14 = bf16[1,128,2048]{2,1,0:T(8,128)(2,1)} copy(bf16[1,128,2048]{2,1,0:T(8,128)(2,1)} %bitcast.5) | data formatting | bytes 1048576
  122.2 1.4 %copy.15 = f32[64,128]{1,0:T(8,128)} copy(f32[64,128]{1,0:T(8,128)} %get-tuple-element.21) | data formatting | bytes 65536
  123.6 1.4 %copy.16 = f32[64,128]{1,0:T(8,128)} copy(f32[64,128]{1,0:T(8,128)} %get-tuple-element.22) | data formatting | bytes 65536
  124.9 1.7 %copy.17 = f32[64,1024]{1,0:T(8,128)} copy(f32[64,1024]{1,0:T(8,128)} %get-tuple-element.23) | data formatting | bytes 524288

commit v4 on v3

--- a/solution.py
+++ b/solution.py
@@ -144,7 +144,7 @@
 def attention_kernel(
     wide, outer, inner, r_ref, c_ref, x_ref, got_ref, xb_ref,
     o_ref, fq_ref, fk_ref, va_ref, ah, al, gh, gl, nh, nl, st_ref, gi_ref, pg_ref,
-    send_i, recv_i, send_x, recv_x, send_r, recv_r,
+    send_i, recv_i, send_x, recv_x, send_q, recv_q, send_r, recv_r,
 ):
     blocks, _, tokens = r_ref.shape
     size, me, where = group("seq", outer, inner)
@@ -213,6 +213,17 @@
     zero = jnp.zeros((wide + AUX, feats), F32)
     lax.fori_loop(0, chunks, forward, zero)
 
+    def give(start, count, send, recv):
+        copies = []
+        for k in range(1, size):
+            peer = (me + k) % size
+            src = o_ref.at[peer, pl.ds(start, count)]
+            dst = got_ref.at[me, pl.ds(start, count)]
+            copies.append(push(src, dst, send.at[k], recv.at[k], where(peer)))
+        return copies
+
+    returns = give(0, DK, send_q, recv_q)
+
     def backward(step, state):
         c = chunks - 1 - step
         uk = block(c)[DK : 2 * DK] * 0.5
@@ -225,16 +236,10 @@
         store(c, 2 * DK, gv[:wide])
         gfk = dot2r(fq, ga, (1, 1)) + dot2(held, va, (0, 0))
         store(c, DK, pull(uk, gfk, coef) * 0.5)
-        for t in range(2):
-            peer = 2 * c + t
-
-            @pl.when(peer != me)
-            def _():
-                push(o_ref.at[peer], got_ref.at[me], send_r.at[peer], recv_r.at[me], where(peer))
-
         return state + dot2(gn, fq, (1, 1))
 
     lax.fori_loop(0, chunks, backward, zero)
+    returns += give(DK, DK + wide, send_r, recv_r)
     got_ref[me] = o_ref[me]
     for copy in inside:
         copy.wait()
@@ -244,16 +249,8 @@
     pair.wait()
     for j in range(inner):
         xb_ref[2 * j + 1 - core] = pg_ref[j].astype(BF)
-    for k in range(1, size):
-        peer = (me + k) % size
-        pltpu.make_async_remote_copy(
-            src_ref=o_ref.at[peer],
-            dst_ref=got_ref.at[peer],
-            send_sem=send_r.at[peer],
-            recv_sem=recv_r.at[peer],
-            device_id=where(peer),
-            device_id_type=MESH,
-        ).wait()
+    for copy in returns:
+        copy.wait()
 
 
 def attention(received, tokens_in, wide, outer, inner):
@@ -269,7 +266,7 @@
     group_in = pltpu.VMEM((inner, tokens, width), F32)
     scratch = [pltpu.VMEM(result, F32), feat, feat, grads, square, square, square, square]
     scratch += [grads, grads, group_in, group_in, group_in]
-    scratch += [sems(inner)] * 2 + [sems(1)] * 2 + [sems(blocks)] * 2
+    scratch += [sems(inner)] * 2 + [sems(1)] * 2 + [sems(blocks)] * 4
     return pl.pallas_call(
         functools.partial(attention_kernel, wide, outer, inner),
         out_shape=[
@@ -346,8 +343,8 @@
 
 
 def tail_kernel(
-    outer, inner, pieces, g_ref, xb_ref, wq_hbm, wk_hbm, wv_hbm, gi_ref, oq_ref, ok_ref, ov_ref,
-    wq_ref, wk_ref, wv_ref, jt_ref, jb_ref, gj_ref, ls_ref, lr_ref, fs_ref, os_ref, o_ref,
+    outer, inner, pieces, g_ref, xb_ref, wq_hbm, wk_hbm, wv_hbm, gi_ref, o_ref,
+    wq_ref, wk_ref, wv_ref, jt_ref, jb_ref, gj_ref, ls_ref, lr_ref, fs_ref, os_ref,
     load, send_j, recv_j, send_l, recv_l, send_o, recv_o,
 ):
     loads = []
@@ -433,10 +430,6 @@
     for i, copy in enumerate(lasts):
         copy.wait_recv()
         o_ref[other * pieces + i] = os_ref[i]
-    oq_ref[...] = o_ref[0]
-    ok_ref[...] = o_ref[1]
-    for n in range(H):
-        ov_ref[:, n * DV : (n + 1) * DV] = o_ref[2 + n]
     for row in gathers + reduces + [lasts]:
         for copy in row:
             copy.wait_send()
@@ -457,7 +450,6 @@
         vm(pieces, outer, DV, rows),
         vm(pieces, rows, DV),
         vm(pieces, rows // 2, DV),
-        vm(2 * pieces, rows // 2, DV),
         sems(3),
         sems(pieces, plane), sems(pieces, plane),
         sems(pieces, outer), sems(pieces, outer),
@@ -467,15 +459,36 @@
         functools.partial(tail_kernel, outer, inner, pieces),
         out_shape=[
             jax.ShapeDtypeStruct((length, width), BF),
-            jax.ShapeDtypeStruct((rows // 2, DV), F32),
-            jax.ShapeDtypeStruct((rows // 2, DV), F32),
-            jax.ShapeDtypeStruct((rows // 2, H * DV), F32),
+            jax.ShapeDtypeStruct((2 * pieces, rows // 2, DV), F32),
         ],
         in_specs=[VMEM] * 2 + [HBM] * 3,
-        out_specs=[VMEM] * 4,
+        out_specs=[VMEM] * 2,
         scratch_shapes=scratch,
         compiler_params=params(2),
     )(grads, inside, *weights)
+
+
+def finish_kernel(gi_ref, o_ref, in_ref, oq_ref, ok_ref, ov_ref):
+    in_ref[0] = gi_ref[...]
+    oq_ref[...] = o_ref[0]
+    ok_ref[...] = o_ref[1]
+    for n in range(H):
+        ov_ref[:, n * DV : (n + 1) * DV] = o_ref[2 + n]
+
+
+def finish(grad_in, blocks):
+    _, rows, lanes = blocks.shape
+    return pl.pallas_call(
+        finish_kernel,
+        out_shape=[
+            jax.ShapeDtypeStruct((1,) + grad_in.shape, BF),
+            jax.ShapeDtypeStruct((rows, lanes), F32),
+            jax.ShapeDtypeStruct((rows, lanes), F32),
+            jax.ShapeDtypeStruct((rows, H * lanes), F32),
+        ],
+        in_specs=[VMEM] * 2,
+        out_specs=[VMEM] * 4,
+    )(grad_in, blocks)
 
 
 def body(inputs, cotangent, w_query, w_key, w_value):
@@ -487,8 +500,7 @@
     weights = (w_query, w_key, w_value)
     received = front(tokens, cotangent[0], weights, outer, inner)
     grads, inside = attention(received, tokens, wide, outer, inner)
-    grad_in, grad_wq, grad_wk, grad_wv = tail(grads, inside, weights, outer, inner)
-    return (grad_in[None], grad_wq, grad_wk, grad_wv)
+    return tuple(finish(*tail(grads, inside, weights, outer, inner)))
 
 
 def solution(mesh):

time: 127 us -> 121 us (0.953)
  local copies, waits for them, and re-layouts: 6.3 us -> 0 us
    unnamed x4 -> x0, local copies, waits for them, and re-layouts: 6.3 us -> none
    pallas_call x1, Pallas kernels: 43 us -> 37.2 us  [attention(): pl.pallas_call(functools.partial(attention_kernel, wide, outer, inner), o...]
    pallas_call x1, Pallas kernels: 44 us -> 48.2 us  [tail(): pl.pallas_call(functools.partial(tail_kernel, outer, inner, pieces), out_...]
    pallas_call x0 -> x1, Pallas kernels: none -> 2.06 us  [finish(): pl.pallas_call(finish_kernel, out_shape=[jax.ShapeDtypeStruct((1,) + grad...]
where the time goes in v4:
time: 121 us
  Pallas kernels  120 us (99%)
    pallas_call x1, Pallas kernels, tail(): pl.pallas_call(functools.partial(tail_kernel, outer, inner, pieces), out_...  48.2 us
    pallas_call x1, Pallas kernels, attention(): pl.pallas_call(functools.partial(attention_kernel, wide, outer, inner), o...  37.2 us
    pallas_call x1, Pallas kernels, front(): pl.pallas_call(functools.partial(front_kernel, outer, inner), out_shape=j...  32.6 us

profile of v4, /device:TPU:0, one launch (start us, length us, event | category | flops | bytes accessed | tf_op | source)
XLA Modules:
  0.0 120.8 jit_solution(6320827708486719574)
XLA Ops:
  0.6 32.6 %shard_map.93.r_ref = f32[16,160,128]{2,1,0:T(8,128)} custom-call(bf16[128,2048]{1,0:T(8,128)(2,1)} %bitcast.2, bf16[128,1024]{1,0:T(8,128)(2,1)} %bitcast.4, bf16[2048,128]{1,0:T(8,128)(2,1)} %wq_hbm.3, bf16[2048,128]{1,0:T(8,128)(2,1)} %wk_hbm.3, bf16[2048,1024]{1,0:T(8,128)(2,1)} %wv_hbm.3), custom_call_target="tpu_custom_call" | custom-call | tf_op jit(solution)/shard_map/pallas_call | solution.py:335
  33.3 37.2 %shard_map.94 = (f32[16,96,128]{2,1,0:T(8,128)}, bf16[8,128,512]{2,1,0:T(8,128)(2,1)}) custom-call(f32[16,160,128]{2,1,0:T(8,128)} %shard_map.93.r_ref, f32[192,128]{1,0:T(8,128)} %constant.2.clone.c_ref, bf16[128,2048]{1,0:T(8,128)(2,1)} %bitcast.3), custom_call_target="tpu_custom_call" | custom-call | tf_op jit(solution)/shard_map/pallas_call | solution.py:270
  70.5 48.2 %shard_map.95 = (bf16[128,2048]{1,0:T(8,128)(2,1)}, f32[10,64,128]{2,1,0:T(8,128)}) custom-call(f32[16,96,128]{2,1,0:T(8,128)} %get-tuple-element.8.g_ref, bf16[8,128,512]{2,1,0:T(8,128)(2,1)} %get-tuple-element.9.xb_ref, bf16[2048,128]{1,0:T(8,128)(2,1)} %wq_hbm.3, bf16[2048,128]{1,0:T(8,128)(2,1)} %wk_hbm.3, bf16[2048,1024]{1,0:T(8,128)(2,1)} %wv_hbm.3), custom_call_target="tpu_custom_call" | custom-call | tf_op jit(solution)/shard_map/pallas_call | solution.py:458
  118.7 2.1 %shard_map.96 = (bf16[1,128,2048]{2,1,0:T(8,128)(2,1)}, f32[64,128]{1,0:T(8,128)}, f32[64,128]{1,0:T(8,128)}, f32[64,1024]{1,0:T(8,128)}) custom-call(bf16[128,2048]{1,0:T(8,128)(2,1)} %get-tuple-element.10.gi_ref, f32[10,64,128]{2,1,0:T(8,128)} %get-tuple-element.11.o_ref), custom_call_target="tpu_custom_call" | custom-call | tf_op jit(solution)/shard_map/pallas_call | solution.py:481
